TPU v7x, 32 devices: a whole 2x2x4 slice. The times are simulated.
32 devices in a mesh: patch: 8 (over y, x, core), rhs: 4 (over z).
Axes of the slice: x: 2, y: 2, z: 4, core: 2. Of those that a mesh axis runs over, the one named last changes fastest.
Arguments:
- rhs_vectors: float32 [64, 16, 384], P('patch', 'rhs'), may hold values from -8 to 8
- near_blocks: bfloat16 [64, 4, 384, 384], P('patch'), may hold values from -1 to 5, as said below
- neighbours: int32 [64, 4], P('patch'), may hold values from 0 to 63, as said below
- up_maps: float32 [64, 64, 384], P('patch'), may hold values from -0.3125 to 0.3125
- shift_up: float32 [64, 64, 64], P('patch'), may hold values from -0.25 to 0.25
- far_lists: int32 [8, 4], P('patch'), may hold values from 0 to 7, as said below
- translations: float32 [8, 4, 64, 64], P('patch'), may hold values from -0.375 to 0.375
- shift_down: float32 [64, 64, 64], P('patch'), may hold values from -0.75 to 0.75
- down_maps: float32 [64, 384, 64], P('patch'), may hold values from -0.375 to 0.375
Outputs:
- solution: float32 [64, 16, 384], P('patch', 'rhs')
- residual: float32 [64, 16, 384], P('patch', 'rhs')
Inputs may be any that keep to these rules, and one draw needn't show every extreme that they name: `neighbours`: entry 0 of each row is the patch itself; every other entry names a patch of the same cell or of the cell just before or just after it, cyclically. `far_lists`: entry 0 of each row names the cell just before or just after the row's own cell, cyclically, and for cell 0 the cell just before it; every other entry names a cell other than the row's own. `near_blocks`: the blocks keep the operator's symmetric part positive definite.
All inputs are finite; a program needn't handle non-finite values.
Results may differ from a plain program's by a relative error of at most 0.008.
The roundings to bfloat16 on the way count: a program that leaves them out, or rounds other values in their place, can miss the bound.
Values may be sent and summed in bfloat16 or wider, within the bound.
A program may use at most 64 MiB of HBM per device.

v0:
```python
import jax
import jax.numpy as jnp
from jax import lax
from jax.sharding import PartitionSpec as P

ITERS = 2
HIGH = lax.Precision.HIGHEST


def with_halo(block, sides, width):
    for axis, dim in sides:
        count = lax.axis_size(axis)
        forward = [(i, i + 1) for i in range(count - 1)]
        forward.append((count - 1, 0))
        backward = [(target, source) for source, target in forward]
        low = lax.ppermute(
            lax.slice_in_dim(block, block.shape[dim] - width, None, axis=dim), axis, forward
        )
        high = lax.ppermute(lax.slice_in_dim(block, 0, width, axis=dim), axis, backward)
        block = jnp.concatenate([low, block, high], axis=dim)
    return block


def spd_solve(matrix, right):
    factor = jnp.linalg.cholesky(matrix)
    return jax.scipy.linalg.cho_solve((factor, True), right)


def gram(left, right):
    return jnp.einsum("pkw,plw->kl", left, right, precision=HIGH)


def mix(field, coeffs):
    return jnp.einsum("pkw,kl->plw", field, coeffs, precision=HIGH)


def residual_sum(residual):
    return lax.psum(gram(residual, residual), "patch")


def apply_operator(
    field,
    near_blocks,
    neighbours,
    up_maps,
    shift_up,
    far_lists,
    translations,
    shift_down,
    down_maps,
):
    patches = field.shape[0]
    count = lax.axis_size("patch")
    first = lax.axis_index("patch") * patches - patches
    rounded = field.astype(jnp.bfloat16)
    widened = with_halo(rounded, (("patch", 0),), patches)
    local_ids = jnp.mod(neighbours - first, patches * count)
    picked = widened[local_ids]
    near = jnp.einsum("pjvw,pjkw->pkv", near_blocks, picked, preferred_element_type=jnp.float32)
    moments = jnp.einsum("pew,pkw->pke", up_maps, field, precision=HIGH)
    cell_moment = jnp.einsum("pfe,pke->kf", shift_up, moments, precision=HIGH)
    sources = far_lists[0]
    table = translations[0]
    piece = lax.all_gather(cell_moment[None], "patch", axis=0, tiled=True)
    labels = jnp.arange(piece.shape[0], dtype=jnp.int32)
    select = (sources[:, None] == labels[None, :]).astype(jnp.float32)
    chosen = jnp.einsum("ji,ike->jke", select, piece, precision=HIGH)
    local_exp = jnp.zeros_like(cell_moment) + jnp.einsum(
        "jfe,jke->kf", table, chosen, precision=HIGH
    )
    patch_exp = jnp.einsum("pfe,ke->pkf", shift_down, local_exp, precision=HIGH)
    far = jnp.einsum("pvf,pkf->pkv", down_maps, patch_exp, precision=HIGH)
    return near + far


def on_device(
    rhs_vectors,
    near_blocks,
    neighbours,
    up_maps,
    shift_up,
    far_lists,
    translations,
    shift_down,
    down_maps,
):
    my_cols = rhs_vectors.shape[1]
    offset = lax.axis_index("rhs") * my_cols
    residual = lax.all_gather(rhs_vectors, "rhs", axis=1, tiled=True)
    solution = jnp.zeros_like(residual)
    direction = residual
    current = jnp.zeros((residual.shape[1], residual.shape[1]), jnp.float32)
    for step in range(ITERS):
        image = apply_operator(
            direction,
            near_blocks,
            neighbours,
            up_maps,
            shift_up,
            far_lists,
            translations,
            shift_down,
            down_maps,
        )
        if step == 0:
            current = residual_sum(residual)
        curve = lax.psum(gram(direction, image), "patch")
        curve = 0.5 * (curve + curve.T)
        alpha = spd_solve(curve, current)
        solution = solution + mix(direction, alpha)
        residual = residual - mix(image, alpha)
        if step + 1 < ITERS:
            following = residual_sum(residual)
            beta = spd_solve(current, following)
            direction = residual + mix(direction, beta)
            current = following
    solution_mine = lax.dynamic_slice_in_dim(solution, offset, my_cols, 1)
    residual_mine = lax.dynamic_slice_in_dim(residual, offset, my_cols, 1)
    return (solution_mine, residual_mine)


def solution(mesh):
    return jax.shard_map(
        on_device,
        mesh=mesh,
        in_specs=(
            P("patch", "rhs", None),
            P("patch", None, None, None),
            P("patch", None),
            P("patch", None, None),
            P("patch", None, None),
            P("patch", None),
            P("patch", None, None, None),
            P("patch", None, None),
            P("patch", None, None),
        ),
        out_specs=(P("patch", "rhs", None), P("patch", "rhs", None)),
        check_vma=False,
    )
```

profile of v0, /device:TPU:0, one launch (start us, length us, event | category | flops | bytes accessed | tf_op | source)
XLA Modules:
  0.0 129.5 jit_solution(5300560113778208520)
XLA Ops:
  0.6 0.9 copy.61
  1.5 15.5 %all_gather.9 = f32[8,16,384]{2,0,1:T(8,128)S(1)} all-gather(f32[8,4,384]{2,0,1:T(8,128)S(1)} %copy.61), channel_id=1, replica_groups=mesh['patch'=8,'rhs'=4] {'rhs'}, dimensions={1}, use_global_device_ids=true | all-gather | bytes 245760 | tf_op jit(solution)/shard_map/all_gather | solution.py:89
  17.0 0.1 collective-permute-start.1
  17.1 0.5 collective-permute-start
  17.6 0.4 convolution_bitcast_fusion.14
  17.9 0.7 compare_select_fusion
  18.7 0.1 copy.63
  18.7 0.1 reshape.17
  18.8 2.1 %fusion.11 = f32[8,16,64]{2,1,0:T(8,128)S(1)} fusion(f32[8,64,384]{2,1,0:T(8,128)} %param.15, f32[8,16,384]{2,0,1:T(8,128)S(1)} %all_gather.9), kind=kOutput, calls=%fused_computation.33 | convolution fusion | flops 37748736 | bytes 1015808 | tf_op jit(solution)/shard_map/pew,pkw->pke/dot_general | solution.py:60
  20.9 1.2 convolution_bitcast_fusion.11
  22.1 9.3 %all-gather = f32[128,64]{1,0:T(8,128)S(1)} all-gather(f32[16,64]{1,0:T(8,128)S(1)} %convolution_bitcast_fusion.11), channel_id=2, replica_groups=mesh['patch'=8,'rhs'=4] {'patch'}, dimensions={0}, use_global_device_ids=true | all-gather | bytes 36864 | tf_op jit(solution)/shard_map/all_gather | solution.py:64
  31.4 0.9 fusion.15
  32.3 1.1 fusion.4
  33.4 1.7 %convolution_bitcast_fusion.6 = f32[8,16,64]{2,1,0:T(8,128)S(1)} fusion(f32[16,64,1]{1,0,2:T(8,128)S(1)} %fusion.4, f32[8,64,64]{2,1,0:T(8,128)} %param.19), kind=kOutput, calls=%fused_computation.12 | convolution fusion | flops 6291456 | bytes 167936 | tf_op jit(solution)/shard_map/pfe,ke->pkf/dot_general | solution.py:71
  35.2 0.6 gather_fusion
  35.9 6.3 %convolution_bitcast_fusion.4 = f32[8,16,384]{2,1,0:T(8,128)S(1)} fusion(bf16[8,4,16,384]{3,2,1,0:T(8,128)(2,1)S(1)} %bitcast.140, bf16[8,4,384,384]{3,2,1,0:T(8,128)(2,1)} %param.13), kind=kOutput, calls=%fused_computation.10 | convolution fusion | flops 150994944 | bytes 10027008 | tf_op jit(solution)/shard_map/pjvw,pjkw->pkv/dot_general | solution.py:59
  42.2 0.6 convolution_add_fusion.1
  42.8 0.4 convolution_bitcast_fusion.15
  43.2 23.6 %all-reduce = (f32[16,16]{0,1:T(8,128)S(1)}, f32[16,16]{1,0:T(8,128)S(1)}) all-reduce(f32[16,16]{0,1:T(8,128)S(1)} %convolution_bitcast_fusion.14, f32[16,16]{1,0:T(8,128)S(1)} %convolution_bitcast_fusion.15), channel_id=1, replica_groups=mesh['patch'=8,'rhs'=4] {'patch'}, use_global_device_ids=true, to_apply=%region_3.5 | all-reduce | flops 512 | bytes 4096 | tf_op jit(solution)/shard_map/psum | solution.py:38
  66.8 0.1 copy.69
  66.9 0.1 copy.70
  67.0 1.5 %cholesky.59 = f32[16,16]{1,0:T(8,128)S(1)} custom-call(f32[16,16]{1,0:T(8,128)S(1)} %fusion.35), custom_call_target="Cholesky" | custom-call | tf_op jit(solution)/shard_map/jit(cholesky)/cholesky | solution.py:25
  68.4 0.6 compare_reduce_fusion.2
  69.1 0.6 fusion.20
  69.8 1.2 custom-call.9
  71.0 0.1 copy.78
  71.0 0.2 fusion.33
  71.3 0.2 convolution_bitcast_fusion.10
  71.5 0.3 fusion.1
  71.8 0.3 convolution_bitcast_fusion.13
  72.1 12.1 %psum.30 = f32[16,16]{1,0:T(8,128)S(1)} all-reduce(f32[16,16]{1,0:T(8,128)S(1)} %convolution_bitcast_fusion.13), channel_id=1, replica_groups=mesh['patch'=8,'rhs'=4] {'patch'}, use_global_device_ids=true, to_apply=%region_4.7 | all-reduce | flops 256 | bytes 2048 | tf_op jit(solution)/shard_map/psum | solution.py:38
  84.2 1.4 %cholesky.70 = f32[16,16]{1,0:T(8,128)S(1)} custom-call(f32[16,16]{1,0:T(8,128)S(1)} %fusion.31), custom_call_target="Cholesky" | custom-call | tf_op jit(solution)/shard_map/jit(cholesky)/cholesky | solution.py:25
  85.7 0.6 compare_reduce_fusion.1
  86.3 0.6 fusion.21
  87.0 1.2 custom-call.10
  88.2 0.2 fusion.29
  88.4 0.2 convolution_bitcast_fusion.9
  88.6 0.3 fusion.43
  89.0 0.1 collective-permute-start.3
  89.0 0.5 collective-permute-start.2
  89.5 0.3 fusion.7
  89.8 0.9 fusion.44
  90.8 0.3 convolution_bitcast_fusion.8
  91.1 9.4 %all-gather.1 = f32[128,64]{1,0:T(8,128)S(1)} all-gather(f32[16,64]{1,0:T(8,128)S(1)} %convolution_bitcast_fusion.8), channel_id=3, replica_groups=mesh['patch'=8,'rhs'=4] {'patch'}, dimensions={0}, use_global_device_ids=true | all-gather | bytes 36864 | tf_op jit(solution)/shard_map/all_gather | solution.py:64
  100.4 0.2 fusion.13
  100.7 0.2 fusion.2
  100.9 0.7 convolution_bitcast_fusion.5
  101.7 0.6 gather_fusion.1
  102.3 6.2 %convolution_bitcast_fusion.3 = f32[8,16,384]{2,1,0:T(8,128)S(1)} fusion(bf16[8,4,16,384]{3,2,1,0:T(8,128)(2,1)S(1)} %bitcast.139, bf16[8,4,384,384]{3,2,1,0:T(8,128)(2,1)} %param.13), kind=kOutput, calls=%fused_computation.9 | convolution fusion | flops 150994944 | bytes 10027008 | tf_op jit(solution)/shard_map/pjvw,pjkw->pkv/dot_general | solution.py:59
  108.5 0.6 convolution_add_fusion
  109.2 0.3 convolution_bitcast_fusion.12
  109.5 13.5 %psum.31 = f32[16,16]{1,0:T(8,128)S(1)} all-reduce(f32[16,16]{1,0:T(8,128)S(1)} %convolution_bitcast_fusion.12), channel_id=1, replica_groups=mesh['patch'=8,'rhs'=4] {'patch'}, use_global_device_ids=true, to_apply=%region_5.8 | all-reduce | flops 256 | bytes 2048 | tf_op jit(solution)/shard_map/psum | solution.py:107
  123.0 0.1 copy.83
  123.0 0.1 copy.84
  123.1 1.5 %cholesky.81 = f32[16,16]{1,0:T(8,128)S(1)} custom-call(f32[16,16]{1,0:T(8,128)S(1)} %fusion.26), custom_call_target="Cholesky" | custom-call | tf_op jit(solution)/shard_map/jit(cholesky)/cholesky | solution.py:25
  124.6 0.6 compare_reduce_fusion
  125.3 0.6 fusion.22
  125.9 1.2 custom-call.11
  127.1 0.2 fusion.24
  127.3 0.2 convolution_bitcast_fusion.7
  127.6 0.3 fusion.45
  127.9 0.3 convolution_bitcast_fusion
  128.2 0.6 dynamic-slice_subtract_fusion
  128.8 0.6 fusion.17
  (28 shorter events, 0.4 us)
Async XLA Ops:
  0.6 41.6 %copy-start = (f32[8,384,64]{1,2,0:T(8,128)S(1)}, f32[8,384,64]{1,2,0:T(8,128)}, u32[]{:S(2)}) copy-start(f32[8,384,64]{1,2,0:T(8,128)} %param.20) | copy-start | bytes 2359300
  17.0 18.1 %collective-permute-start.1 = (bf16[8,16,384]{2,1,0:T(8,128)(2,1)S(1)}, bf16[8,16,384]{2,1,0:T(8,128)(2,1)S(1)}, u32[]{:S(2)}, u32[]{:S(2)}) collective-permute-start(bf16[8,16,384]{2,1,0:T(8,128)(2,1)S(1)} %copy.116), channel_id=1, source_target_pairs={{4,0},{8,4},{12,8},{16,12},{20,16},{24,20},{28,24},{0,28},{5,1},{9... | collective-permute-start | bytes 294920 | tf_op jit(solution)/shard_map/ppermute | solution.py:19
  17.1 18.1 %collective-permute-start = (bf16[8,16,384]{2,1,0:T(8,128)(2,1)S(1)}, bf16[8,16,384]{2,1,0:T(8,128)(2,1)S(1)}, u32[]{:S(2)}, u32[]{:S(2)}) collective-permute-start(bf16[8,16,384]{2,1,0:T(8,128)(2,1)S(1)} %copy.116), channel_id=1, source_target_pairs={{0,4},{4,8},{8,12},{12,16},{16,20},{20,24},{24,28},{28,0},{1,5},{5... | collective-permute-start | bytes 294920 | tf_op jit(solution)/shard_map/ppermute | solution.py:16
  35.8 54.0 %copy-start.1 = (f32[8,64,384]{2,1,0:T(8,128)S(1)}, f32[8,64,384]{2,1,0:T(8,128)}, u32[]{:S(2)}) copy-start(f32[8,64,384]{2,1,0:T(8,128)} %param.15) | copy-start | bytes 2359300
  35.9 54.9 %copy-start.2 = (f32[8,64,64]{2,1,0:T(8,128)S(1)}, f32[8,64,64]{2,1,0:T(8,128)}, u32[]{:S(2)}) copy-start(f32[8,64,64]{2,1,0:T(8,128)} %param.16) | copy-start | bytes 393220
  35.9 64.6 %copy-start.5 = (s32[1,4]{1,0:T(1,128)S(1)}, s32[1,4]{1,0:T(1,128)}, u32[]{:S(2)}) copy-start(s32[1,4]{1,0:T(1,128)} %param.17) | copy-start | bytes 52
  35.9 64.8 %copy-start.4 = (f32[1,4,64,64]{3,2,1,0:T(8,128)S(1)}, f32[1,4,64,64]{3,2,1,0:T(8,128)}, u32[]{:S(2)}) copy-start(f32[1,4,64,64]{3,2,1,0:T(8,128)} %param.18) | copy-start | bytes 196612
  35.9 65.0 %copy-start.3 = (f32[8,64,64]{2,1,0:T(8,128)S(1)}, f32[8,64,64]{2,1,0:T(8,128)}, u32[]{:S(2)}) copy-start(f32[8,64,64]{2,1,0:T(8,128)} %param.19) | copy-start | bytes 393220
  89.0 12.6 %collective-permute-start.3 = (bf16[8,16,384]{2,1,0:T(8,128)(2,1)S(1)}, bf16[8,16,384]{2,1,0:T(8,128)(2,1)S(1)}, u32[]{:S(2)}, u32[]{:S(2)}) collective-permute-start(bf16[8,16,384]{2,1,0:T(8,128)(2,1)S(1)} %get-tuple-element.6), channel_id=1, source_target_pairs={{4,0},{8,4},{12,8},{16,12},{20,16},{24,20},{28,24},{0,28},{5,1},{9... | collective-permute-start | bytes 294920 | tf_op jit(solution)/shard_map/ppermute | solution.py:19
  89.0 12.6 %collective-permute-start.2 = (bf16[8,16,384]{2,1,0:T(8,128)(2,1)S(1)}, bf16[8,16,384]{2,1,0:T(8,128)(2,1)S(1)}, u32[]{:S(2)}, u32[]{:S(2)}) collective-permute-start(bf16[8,16,384]{2,1,0:T(8,128)(2,1)S(1)} %get-tuple-element.6), channel_id=1, source_target_pairs={{0,4},{4,8},{8,12},{12,16},{16,20},{20,24},{24,28},{28,0},{1,5},{5... | collective-permute-start | bytes 294920 | tf_op jit(solution)/shard_map/ppermute | solution.py:16
where the time goes:
time: 130 us; the launch traced here: 129 us
  blocking collectives  83.3 us (64%)
  matrix products  27.2 us (21%)
  other arithmetic  14.2 us (11%)
  local copies, waits for them, and re-layouts  2.76 us (2%)
    psum x2, blocking collectives, residual_sum(): return lax.psum(gram(residual, residual), 'patch')  35.7 us
    all_gather x2, blocking collectives, apply_operator(): piece = lax.all_gather(cell_moment[None], 'patch', axis=0, tiled=True)  18.7 us
    all_gather x1, blocking collectives, on_device(): residual = lax.all_gather(rhs_vectors, 'rhs', axis=1, tiled=True)  15.5 us
    psum x1, blocking collectives, on_device(): curve = lax.psum(gram(direction, image), 'patch')  13.5 us
    dot_general x2, matrix products, apply_operator(): jnp.einsum('pjvw,pjkw->pkv', near_blocks, picked, preferred_element_type=...  12.5 us
    another operation x9, other arithmetic, spd_solve(): factor = jnp.linalg.cholesky(matrix)  6.39 us
    another operation x6, other arithmetic, spd_solve(): return jax.scipy.linalg.cho_solve((factor, True), right)  5.63 us
    dot_general x2, matrix products, apply_operator(): moments = jnp.einsum('pew,pkw->pke', up_maps, field, precision=HIGH)  2.99 us
  transfers between devices with their start and end apart: 4, of which 0 were waited for; matrix products, arithmetic and copies ran while one was open for 8% of the time, Pallas kernels for 0%

commit v1 on v0

--- a/solution.py
+++ b/solution.py
@@ -35,7 +35,7 @@
 
 
 def residual_sum(residual):
-    return lax.psum(gram(residual, residual), "patch")
+    return jnp.sum(lax.all_gather(gram(residual, residual), "patch"), axis=0)
 
 
 def apply_operator(

time: 130 us -> 126 us (0.969)
  blocking collectives: 83.3 us -> 78.8 us
    psum x2 -> x0, blocking collectives: 35.7 us -> none  [residual_sum(): return lax.psum(gram(residual, residual), 'patch')]
    all_gather x0 -> x2, blocking collectives: none -> 17.6 us  [residual_sum(): return jnp.sum(lax.all_gather(gram(residual, residual), 'patch'), axis=0)]
    psum x1 -> x2, blocking collectives: 13.5 us -> 27 us  [on_device(): curve = lax.psum(gram(direction, image), 'patch')]
    ppermute x2, starting transfers between devices: 0.12 us -> 1.52 us  [with_halo(): lax.ppermute(lax.slice_in_dim(block, 0, width, axis=dim), axis, backward)]
  transfers between devices with their start and end apart: 4 -> 4, of which waited for: 0 -> 0; matrix products, arithmetic and copies ran while one was open for 8% -> 12% of each run, Pallas kernels for 0% -> 0%
where the time goes in v1:
time: 126 us
  blocking collectives  78.8 us (63%)
  matrix products  27.2 us (22%)
  other arithmetic  14.2 us (11%)
  local copies, waits for them, and re-layouts  2.76 us (2%)
  starting transfers between devices  2.02 us (2%)
    psum x2, blocking collectives, on_device(): curve = lax.psum(gram(direction, image), 'patch')  27 us
    all_gather x2, blocking collectives, apply_operator(): piece = lax.all_gather(cell_moment[None], 'patch', axis=0, tiled=True)  18.8 us
    all_gather x2, blocking collectives, residual_sum(): return jnp.sum(lax.all_gather(gram(residual, residual), 'patch'), axis=0)  17.6 us
    all_gather x1, blocking collectives, on_device(): residual = lax.all_gather(rhs_vectors, 'rhs', axis=1, tiled=True)  15.5 us
    dot_general x2, matrix products, apply_operator(): jnp.einsum('pjvw,pjkw->pkv', near_blocks, picked, preferred_element_type=...  12.5 us
    another operation x9, other arithmetic, spd_solve(): factor = jnp.linalg.cholesky(matrix)  6.39 us
    another operation x6, other arithmetic, spd_solve(): return jax.scipy.linalg.cho_solve((factor, True), right)  5.63 us
    dot_general x2, matrix products, apply_operator(): moments = jnp.einsum('pew,pkw->pke', up_maps, field, precision=HIGH)  2.99 us
  transfers between devices with their start and end apart: 4, of which 0 were waited for; matrix products, arithmetic and copies ran while one was open for 12% of the time, Pallas kernels for 0%

profile of v1, /device:TPU:0, one launch (start us, length us, event | category | flops | bytes accessed | tf_op | source)
XLA Modules:
  0.0 125.9 jit_solution(17562090675996968210)
XLA Ops:
  0.6 0.9 copy.58
  1.5 15.5 %all_gather.21 = f32[8,16,384]{2,0,1:T(8,128)S(1)} all-gather(f32[8,4,384]{2,0,1:T(8,128)S(1)} %copy.58), channel_id=1, replica_groups=mesh['patch'=8,'rhs'=4] {'rhs'}, dimensions={1}, use_global_device_ids=true | all-gather | bytes 245760 | tf_op jit(solution)/shard_map/all_gather | solution.py:89
  17.0 0.1 collective-permute-start.1
  17.1 0.5 collective-permute-start
  17.6 0.3 convolution_bitcast_fusion.14
  17.9 9.3 %all-gather.1 = f32[128,16]{1,0:T(8,128)S(1)} all-gather(f32[16,16]{1,0:T(8,128)S(1)} %convolution_bitcast_fusion.14), channel_id=3, replica_groups=mesh['patch'=8,'rhs'=4] {'patch'}, dimensions={0}, use_global_device_ids=true | all-gather | bytes 9216 | tf_op jit(solution)/shard_map/all_gather | solution.py:38
  27.2 0.7 compare_select_fusion
  27.9 0.1 copy.60
  28.0 0.1 reshape.17
  28.1 2.1 %fusion.11 = f32[8,16,64]{2,1,0:T(8,128)S(1)} fusion(f32[8,64,384]{2,1,0:T(8,128)} %param.15, f32[8,16,384]{2,0,1:T(8,128)S(1)} %all_gather.21), kind=kOutput, calls=%fused_computation.33 | convolution fusion | flops 37748736 | bytes 1015808 | tf_op jit(solution)/shard_map/pew,pkw->pke/dot_general | solution.py:60
  30.1 1.2 convolution_bitcast_fusion.11
  31.4 9.3 %all-gather = f32[128,64]{1,0:T(8,128)S(1)} all-gather(f32[16,64]{1,0:T(8,128)S(1)} %convolution_bitcast_fusion.11), channel_id=2, replica_groups=mesh['patch'=8,'rhs'=4] {'patch'}, dimensions={0}, use_global_device_ids=true | all-gather | bytes 36864 | tf_op jit(solution)/shard_map/all_gather | solution.py:64
  40.6 0.1 copy.74
  40.7 1.5 %cholesky.70 = f32[16,16]{1,0:T(8,128)S(1)} custom-call(f32[16,16]{1,0:T(8,128)S(1)} %fusion.31), custom_call_target="Cholesky" | custom-call | tf_op jit(solution)/shard_map/jit(cholesky)/cholesky | solution.py:25
  42.2 0.6 compare_reduce_fusion.1
  42.8 0.6 fusion.21
  43.5 1.2 custom-call.10
  44.7 0.9 fusion.15
  45.6 1.1 fusion.4
  46.7 1.7 %convolution_bitcast_fusion.6 = f32[8,16,64]{2,1,0:T(8,128)S(1)} fusion(f32[16,64,1]{1,0,2:T(8,128)S(1)} %fusion.4, f32[8,64,64]{2,1,0:T(8,128)} %param.19), kind=kOutput, calls=%fused_computation.12 | convolution fusion | flops 6291456 | bytes 167936 | tf_op jit(solution)/shard_map/pfe,ke->pkf/dot_general | solution.py:71
  48.5 0.6 gather_fusion
  49.2 6.3 %convolution_bitcast_fusion.4 = f32[8,16,384]{2,1,0:T(8,128)S(1)} fusion(bf16[8,4,16,384]{3,2,1,0:T(8,128)(2,1)S(1)} %bitcast.142, bf16[8,4,384,384]{3,2,1,0:T(8,128)(2,1)} %param.13), kind=kOutput, calls=%fused_computation.10 | convolution fusion | flops 150994944 | bytes 10027008 | tf_op jit(solution)/shard_map/pjvw,pjkw->pkv/dot_general | solution.py:59
  55.5 0.6 convolution_add_fusion.1
  56.1 0.4 convolution_bitcast_fusion.15
  56.5 13.5 %psum.14 = f32[16,16]{1,0:T(8,128)S(1)} all-reduce(f32[16,16]{1,0:T(8,128)S(1)} %convolution_bitcast_fusion.15), channel_id=1, replica_groups=mesh['patch'=8,'rhs'=4] {'patch'}, use_global_device_ids=true, to_apply=%region_0.1 | all-reduce | flops 256 | bytes 2048 | tf_op jit(solution)/shard_map/psum | solution.py:107
  70.0 0.1 copy.66
  70.1 0.1 copy.67
  70.1 1.5 %cholesky.59 = f32[16,16]{1,0:T(8,128)S(1)} custom-call(f32[16,16]{1,0:T(8,128)S(1)} %fusion.35), custom_call_target="Cholesky" | custom-call | tf_op jit(solution)/shard_map/jit(cholesky)/cholesky | solution.py:25
  71.6 0.6 compare_reduce_fusion.2
  72.3 0.6 fusion.20
  72.9 1.2 custom-call.9
  74.2 0.2 fusion.33
  74.4 0.2 convolution_bitcast_fusion.10
  74.6 0.3 fusion.1
  74.9 0.3 convolution_bitcast_fusion.13
  75.2 8.3 %all-gather.2 = f32[128,16]{1,0:T(8,128)S(1)} all-gather(f32[16,16]{1,0:T(8,128)S(1)} %convolution_bitcast_fusion.13), channel_id=4, replica_groups=mesh['patch'=8,'rhs'=4] {'patch'}, dimensions={0}, use_global_device_ids=true | all-gather | bytes 9216 | tf_op jit(solution)/shard_map/all_gather | solution.py:38
  83.6 0.2 fusion.29
  83.8 0.2 convolution_bitcast_fusion.9
  84.0 0.3 fusion.43
  84.3 1.5 %collective-permute-start.3 = (bf16[8,16,384]{2,1,0:T(8,128)(2,1)S(1)}, bf16[8,16,384]{2,1,0:T(8,128)(2,1)S(1)}, u32[]{:S(2)}, u32[]{:S(2)}) collective-permute-start(bf16[8,16,384]{2,1,0:T(8,128)(2,1)S(1)} %get-tuple-element.4), channel_id=1, source_target_pairs={{4,0},{8,4},{12,8},{16,12},{20,16},{24,20},{28,24},{0,28},{5,1},{9... | collective-permute-start | bytes 294920 | tf_op jit(solution)/shard_map/ppermute | solution.py:19
  85.7 0.3 fusion.7
  86.1 0.9 fusion.44
  87.0 0.3 convolution_bitcast_fusion.8
  87.3 9.5 %all-gather.3 = f32[128,64]{1,0:T(8,128)S(1)} all-gather(f32[16,64]{1,0:T(8,128)S(1)} %convolution_bitcast_fusion.8), channel_id=5, replica_groups=mesh['patch'=8,'rhs'=4] {'patch'}, dimensions={0}, use_global_device_ids=true | all-gather | bytes 36864 | tf_op jit(solution)/shard_map/all_gather | solution.py:64
  96.8 0.2 fusion.13
  97.0 0.2 fusion.2
  97.2 0.7 convolution_bitcast_fusion.5
  98.1 0.6 gather_fusion.1
  98.7 6.2 %convolution_bitcast_fusion.3 = f32[8,16,384]{2,1,0:T(8,128)S(1)} fusion(bf16[8,4,16,384]{3,2,1,0:T(8,128)(2,1)S(1)} %bitcast.141, bf16[8,4,384,384]{3,2,1,0:T(8,128)(2,1)} %param.13), kind=kOutput, calls=%fused_computation.9 | convolution fusion | flops 150994944 | bytes 10027008 | tf_op jit(solution)/shard_map/pjvw,pjkw->pkv/dot_general | solution.py:59
  104.9 0.6 convolution_add_fusion
  105.5 0.3 convolution_bitcast_fusion.12
  105.9 13.5 %psum.15 = f32[16,16]{1,0:T(8,128)S(1)} all-reduce(f32[16,16]{1,0:T(8,128)S(1)} %convolution_bitcast_fusion.12), channel_id=1, replica_groups=mesh['patch'=8,'rhs'=4] {'patch'}, use_global_device_ids=true, to_apply=%region_5.8 | all-reduce | flops 256 | bytes 2048 | tf_op jit(solution)/shard_map/psum | solution.py:107
  119.4 0.1 copy.79
  119.4 0.1 copy.80
  119.5 1.5 %cholesky.81 = f32[16,16]{1,0:T(8,128)S(1)} custom-call(f32[16,16]{1,0:T(8,128)S(1)} %fusion.26), custom_call_target="Cholesky" | custom-call | tf_op jit(solution)/shard_map/jit(cholesky)/cholesky | solution.py:25
  121.0 0.6 compare_reduce_fusion
  121.7 0.6 fusion.22
  122.3 1.2 custom-call.11
  123.5 0.2 fusion.24
  123.7 0.2 convolution_bitcast_fusion.7
  123.9 0.3 fusion.45
  124.3 0.3 convolution_bitcast_fusion
  124.6 0.6 dynamic-slice_subtract_fusion
  125.2 0.6 fusion.17
  (31 shorter events, 0.4 us)
Async XLA Ops:
  0.6 54.9 %copy-start = (f32[8,384,64]{1,2,0:T(8,128)S(1)}, f32[8,384,64]{1,2,0:T(8,128)}, u32[]{:S(2)}) copy-start(f32[8,384,64]{1,2,0:T(8,128)} %param.20) | copy-start | bytes 2359300
  17.0 31.4 %collective-permute-start.1 = (bf16[8,16,384]{2,1,0:T(8,128)(2,1)S(1)}, bf16[8,16,384]{2,1,0:T(8,128)(2,1)S(1)}, u32[]{:S(2)}, u32[]{:S(2)}) collective-permute-start(bf16[8,16,384]{2,1,0:T(8,128)(2,1)S(1)} %copy.110), channel_id=1, source_target_pairs={{4,0},{8,4},{12,8},{16,12},{20,16},{24,20},{28,24},{0,28},{5,1},{9... | collective-permute-start | bytes 294920 | tf_op jit(solution)/shard_map/ppermute | solution.py:19
  17.1 31.4 %collective-permute-start = (bf16[8,16,384]{2,1,0:T(8,128)(2,1)S(1)}, bf16[8,16,384]{2,1,0:T(8,128)(2,1)S(1)}, u32[]{:S(2)}, u32[]{:S(2)}) collective-permute-start(bf16[8,16,384]{2,1,0:T(8,128)(2,1)S(1)} %copy.110), channel_id=1, source_target_pairs={{0,4},{4,8},{8,12},{12,16},{16,20},{20,24},{24,28},{28,0},{1,5},{5... | collective-permute-start | bytes 294920 | tf_op jit(solution)/shard_map/ppermute | solution.py:16
  49.1 36.9 %copy-start.1 = (f32[8,64,384]{2,1,0:T(8,128)S(1)}, f32[8,64,384]{2,1,0:T(8,128)}, u32[]{:S(2)}) copy-start(f32[8,64,384]{2,1,0:T(8,128)} %param.15) | copy-start | bytes 2359300
  49.2 37.8 %copy-start.2 = (f32[8,64,64]{2,1,0:T(8,128)S(1)}, f32[8,64,64]{2,1,0:T(8,128)}, u32[]{:S(2)}) copy-start(f32[8,64,64]{2,1,0:T(8,128)} %param.16) | copy-start | bytes 393220
  49.2 47.6 %copy-start.5 = (s32[1,4]{1,0:T(1,128)S(1)}, s32[1,4]{1,0:T(1,128)}, u32[]{:S(2)}) copy-start(s32[1,4]{1,0:T(1,128)} %param.17) | copy-start | bytes 52
  49.2 47.8 %copy-start.4 = (f32[1,4,64,64]{3,2,1,0:T(8,128)S(1)}, f32[1,4,64,64]{3,2,1,0:T(8,128)}, u32[]{:S(2)}) copy-start(f32[1,4,64,64]{3,2,1,0:T(8,128)} %param.18) | copy-start | bytes 196612
  49.2 48.0 %copy-start.3 = (f32[8,64,64]{2,1,0:T(8,128)S(1)}, f32[8,64,64]{2,1,0:T(8,128)}, u32[]{:S(2)}) copy-start(f32[8,64,64]{2,1,0:T(8,128)} %param.19) | copy-start | bytes 393220
  84.3 13.7 %collective-permute-start.3 = (bf16[8,16,384]{2,1,0:T(8,128)(2,1)S(1)}, bf16[8,16,384]{2,1,0:T(8,128)(2,1)S(1)}, u32[]{:S(2)}, u32[]{:S(2)}) collective-permute-start(bf16[8,16,384]{2,1,0:T(8,128)(2,1)S(1)} %get-tuple-element.4), channel_id=1, source_target_pairs={{4,0},{8,4},{12,8},{16,12},{20,16},{24,20},{28,24},{0,28},{5,1},{9... | collective-permute-start | bytes 294920 | tf_op jit(solution)/shard_map/ppermute | solution.py:19
  85.7 12.3 %collective-permute-start.2 = (bf16[8,16,384]{2,1,0:T(8,128)(2,1)S(1)}, bf16[8,16,384]{2,1,0:T(8,128)(2,1)S(1)}, u32[]{:S(2)}, u32[]{:S(2)}) collective-permute-start(bf16[8,16,384]{2,1,0:T(8,128)(2,1)S(1)} %get-tuple-element.4), channel_id=1, source_target_pairs={{0,4},{4,8},{8,12},{12,16},{16,20},{20,24},{24,28},{28,0},{1,5},{5... | collective-permute-start | bytes 294920 | tf_op jit(solution)/shard_map/ppermute | solution.py:16
